TPU v7x, 32 devices: a whole 2x2x4 slice. The times are simulated.
32 devices in a mesh: groups: 2 (over y), rows: 4 (over z), cols: 2 (over x), sub: 2 (over core).
Axes of the slice: x: 2, y: 2, z: 4, core: 2. Of those that a mesh axis runs over, the one named last changes fastest.
Arguments:
- tile_index: int32 [64, 2], P(('groups', 'rows', 'cols', 'sub')), parts along dimension 0, may hold values from 0 to 7, as said below
- tile_values: bfloat16 [64, 256, 256], P(('groups', 'rows', 'cols', 'sub')), parts along dimension 0, may hold values from -0.125 to 0.125
- onsite_energy: float32 [4096], P(('groups', 'rows', 'cols')), parts along dimension 0, may hold values from 0.5 to 4
- start_block: float32 [4096, 64], P(('groups', 'rows', 'cols')), parts along dimension 0, may hold values from -6 to 6
- previous_block: float32 [4096, 64], P(('groups', 'rows', 'cols')), parts along dimension 0, may hold values from -6 to 6
- previous_coupling: float32 [128, 64], P('groups'), parts along dimension 0, may hold values from -0.6 to 0.6
- stored_basis: float32 [8, 4096, 64], P('sub', ('groups', 'rows', 'cols')), parts along dimension 1, may hold values from -6 to 6
Outputs:
- new_blocks: float32 [1, 4096, 64], P(None, ('groups', 'rows', 'cols')), parts along dimension 1
- diagonal_blocks: float32 [1, 128, 64], P(None, 'groups'), parts along dimension 1
- coupling_blocks: float32 [1, 128, 64], P(None, 'groups'), parts along dimension 1
There are 2 independent parts, one for each index of `groups`. A program takes and returns all parts, laid end to end along the dimension named above; each array names one. Nothing has to cross between parts.
Inputs may be any that keep to these rules, and one draw needn't show every extreme that they name: `tile_index`: tile rows of a device's tiles lie in the rows of the operator that the device's index of rows and cols holds; tile columns lie in the rows held by some index of rows with the same index of cols. Tiles may repeat.
All inputs are finite; a program needn't handle non-finite values.
Results may differ from a plain program's by a relative error of at most 0.0019.
Values may be sent and summed in bfloat16 or wider, within the bound.
A program may use at most 64 MiB of HBM per device.

v0:
```python
import jax
import jax.numpy as jnp
from jax import lax
from jax.sharding import PartitionSpec as P

BLOCK = 64
TILE = 256
highest = lax.Precision.HIGHEST


def apply_operator(tile_index, tile_values, onsite_energy, current):
    local_rows = current.shape[0]
    tile_rows = local_rows // TILE
    band_count = lax.axis_size("rows")
    column_count = lax.axis_size("cols")
    narrow = current.astype(jnp.bfloat16)
    own_tiles = narrow.reshape(tile_rows, TILE, BLOCK)
    local_row = tile_index[:, 0] % tile_rows
    column = tile_index[:, 1]
    source = column // tile_rows // column_count * tile_rows + column % tile_rows
    gathered = lax.all_gather(own_tiles, "rows", axis=0, tiled=True)
    pulled = jnp.einsum(
        "kab,kbn->kan", tile_values, gathered[source], preferred_element_type=jnp.float32
    )
    pushed = jnp.einsum(
        "kab,kan->kbn", tile_values, own_tiles[local_row], preferred_element_type=jnp.float32
    )
    slot_count = band_count * tile_rows
    slot_range = jnp.arange(slot_count, dtype=jnp.int32)
    push_onehot = (source[None, :] == slot_range[:, None]).astype(jnp.float32)
    terms = jnp.einsum("sk,kbn->sbn", push_onehot, pushed, precision=highest)
    received = lax.psum_scatter(terms, "rows", scatter_dimension=0, tiled=True)
    row_onehot = (local_row[None, :] == jnp.arange(tile_rows, dtype=jnp.int32)[:, None]).astype(
        jnp.float32
    )
    partial_total = received + jnp.einsum("tk,kan->tan", row_onehot, pulled, precision=highest)
    total = lax.psum(partial_total, "sub")
    return total.reshape(local_rows, BLOCK) + onsite_energy[:, None] * current


def local(
    tile_index,
    tile_values,
    onsite_energy,
    start_block,
    previous_block,
    previous_coupling,
    stored_basis,
):
    local_rows = start_block.shape[0]
    total_rows = local_rows * lax.axis_size("rows") * lax.axis_size("cols")
    coupling = jnp.triu(previous_coupling)
    correlation_local = jnp.einsum("kib,ic->kbc", stored_basis, start_block, precision=highest)
    correlation = lax.psum(correlation_local, ("rows", "cols")) / total_rows
    images = apply_operator(tile_index, tile_values, onsite_energy, start_block)
    images = images - jnp.dot(previous_block, coupling.T, precision=highest)
    diagonal_local = jnp.dot(start_block.T, images, precision=highest)
    stored_local = jnp.einsum("kib,ic->kbc", stored_basis, images, precision=highest)
    raw_diagonal, raw_stored = lax.psum((diagonal_local, stored_local), ("rows", "cols"))
    diagonal = raw_diagonal / total_rows
    projection = raw_stored / total_rows - jnp.einsum(
        "kbc,cd->kbd", correlation, diagonal, precision=highest
    )
    images = images - jnp.dot(start_block, diagonal, precision=highest)
    removal_local = jnp.einsum("kib,kbc->ic", stored_basis, projection, precision=highest)
    removal = lax.psum(removal_local, "sub")
    images = images - removal
    gram_local = jnp.dot(images.T, images, precision=highest)
    gram = lax.psum(gram_local, ("rows", "cols")) / total_rows
    lower_factor = jnp.linalg.cholesky(gram)
    following = lax.linalg.triangular_solve(
        lower_factor, images, left_side=False, lower=True, transpose_a=True
    )
    new_list = [following]
    diagonal_list = [diagonal]
    coupling_list = [lower_factor.T]
    return (jnp.stack(new_list), jnp.stack(diagonal_list), jnp.stack(coupling_list))


def solution(mesh):
    return jax.shard_map(
        local,
        mesh=mesh,
        in_specs=(
            P(("groups", "rows", "cols", "sub"), None),
            P(("groups", "rows", "cols", "sub"), None, None),
            P(("groups", "rows", "cols")),
            P(("groups", "rows", "cols"), None),
            P(("groups", "rows", "cols"), None),
            P("groups", None),
            P("sub", ("groups", "rows", "cols"), None),
        ),
        out_specs=(
            P(None, ("groups", "rows", "cols"), None),
            P(None, "groups", None),
            P(None, "groups", None),
        ),
        check_vma=False,
    )
```

profile of v0, /device:TPU:0, one launch (start us, length us, event | category | flops | bytes accessed | tf_op | source)
XLA Modules:
  0.0 217.6 jit_solution(17785886655713540770)
XLA Ops:
  7.2 0.9 convert_element_type.2
  8.1 0.9 fusion.27
  9.0 0.2 fusion.15
  9.2 0.5 fusion.5
  9.7 0.8 copy.31
  10.6 15.6 %all-gather = bf16[1024,64]{0,1:T(8,128)(2,1)S(1)} all-gather(bf16[256,64]{0,1:T(8,128)(2,1)S(1)} %convert_element_type.2), channel_id=2, replica_groups=mesh['groups'=2,'rows'=4,'cols'=2,'sub'=2] {'rows'}, dimensions={0}, use_global_device_ids=true | all-gather | bytes 163840 | tf_op jit(solution)/shard_map/all_gather | solution.py:21
  26.2 0.6 gather_fusion
  26.8 0.2 convolution_bitcast_fusion.1
  27.0 9.0 %fusion.3 = f32[1,256,64]{0,1,2:T(8,128)} fusion(f32[2,256,64]{1,2,0:T(8,128)S(1)} %convolution_bitcast_fusion.1), kind=kOutput, calls=%fused_computation.13 | convolution fusion | flops 393216 | bytes 196608 | tf_op jit(solution)/shard_map/tk,kan->tan/dot_general | solution.py:36
  36.0 5.2 %copy.42 = f32[1,256,64]{1,2,0:T(8,128)S(1)} copy(f32[1,256,64]{0,1,2:T(8,128)} %fusion.3) | data formatting | bytes 131072 | tf_op jit(solution)/shard_map/tk,kan->tan/dot_general | solution.py:36
  41.2 1.2 fusion.8
  42.4 1.5 add_bitcast_fusion
  43.9 18.8 %all-reduce.5.cloned.1.call-done = f32[256,64]{0,1:T(8,128)} async-done(((f32[256,64]{0,1:T(8,128)}), f32[256,64]{0,1:T(8,128)}) %all-reduce.5.cloned.1.call-update) | async-done | bytes 65552 | tf_op jit(solution)/shard_map/psum | solution.py:37
  62.8 1.1 fusion.2
  63.9 1.2 convolution_bitcast_fusion
  65.1 0.2 convolution_bitcast_fusion.6
  65.3 37.4 %psum.43 = f32[64,64]{0,1:T(8,128)S(1)} all-reduce(f32[64,64]{0,1:T(8,128)S(1)} %convolution_bitcast_fusion.6), channel_id=1, replica_groups=mesh['groups'=2,'rows'=4,'cols'=2,'sub'=2] {'rows','cols'}, use_global_device_ids=true, to_apply=%region_2.3 | all-reduce | flops 4096 | bytes 32768 | tf_op jit(solution)/shard_map/psum | solution.py:59
  102.7 36.2 %all-reduce.9.cloned.1.call-done = (f32[4,64,64]{1,2,0:T(8,128)}, f32[4,64,64]{1,2,0:T(8,128)}) async-done(((f32[4,64,64]{1,2,0:T(8,128)}, f32[4,64,64]{1,2,0:T(8,128)}), (f32[4,64,64]{1,2,0:T(8,128)}, f32[4,64,64]{1,2,0:T(8,128)})) %all-reduce.9.cloned.1.call-update) | async-done | bytes 131088 | tf_op jit(solution)/shard_map/psum | solution.py:54
  138.9 1.2 convolution_subtract_fusion
  140.1 0.9 convolution_bitcast_fusion.5
  141.1 0.7 copy.39
  141.8 16.8 %all-reduce.7.cloned.1.call-done = f32[256,64]{0,1:T(8,128)} async-done(((f32[256,64]{0,1:T(8,128)}), f32[256,64]{0,1:T(8,128)}) %all-reduce.7.cloned.1.call-update) | async-done | bytes 65552 | tf_op jit(solution)/shard_map/psum | solution.py:66
  158.6 1.0 fusion.1
  159.7 0.2 fusion.35
  159.9 37.4 %psum.47 = f32[64,64]{0,1:T(8,128)S(1)} all-reduce(f32[64,64]{0,1:T(8,128)S(1)} %fusion.35), channel_id=1, replica_groups=mesh['groups'=2,'rows'=4,'cols'=2,'sub'=2] {'rows','cols'}, use_global_device_ids=true, to_apply=%region_6.7 | all-reduce | flops 4096 | bytes 32768 | tf_op jit(solution)/shard_map/psum | solution.py:69
  197.3 0.1 copy.38
  197.4 5.8 %cholesky.15 = f32[64,64]{1,0:T(8,128)S(1)} custom-call(f32[64,64]{1,0:T(8,128)S(1)} %fusion.13), custom_call_target="Cholesky" | custom-call | tf_op jit(solution)/shard_map/jit(cholesky)/cholesky | solution.py:70
  203.3 0.6 compare_reduce_fusion
  203.9 0.7 fusion.20
  204.6 4.9 %custom-call.6 = f32[1,64,64]{1,2,0:T(8,128)S(1)} custom-call(f32[1,64,64]{2,1,0:T(8,128)S(1)} %get-tuple-element.20), custom_call_target="InvertDiagBlocksLowerTriangular" | custom-call | tf_op jit(solution)/shard_map/triangular_solve | solution.py:71
  209.5 0.9 convolution_bitcast_fusion.2
  210.4 0.7 copy.40
  (29 shorter events, 0.4 us)
Async XLA Ops:
  7.2 1.9 copy-start
  7.2 35.2 %reduce-scatter.2.cloned.1.call-start = ((), (), s32[]{:S(2)}) async-start(), calls=%async_computation.1 | async-start | bytes 327680 | tf_op jit(solution)/shard_map/reduce_scatter | solution.py:32
  10.5 52.2 %all-reduce.5.cloned.1.call-start = ((), (), s32[]{:S(2)}) async-start(), calls=%async_computation.2 | async-start | bytes 131072 | tf_op jit(solution)/shard_map/psum | solution.py:37
  27.0 14.2 %copy-start.1 = (f32[4,256,64]{1,2,0:T(8,128)S(1)}, f32[4,256,64]{1,2,0:T(8,128)}, u32[]{:S(2)}) copy-start(f32[4,256,64]{1,2,0:T(8,128)} %param.13) | copy-start | bytes 786436
  27.0 14.2 %copy-start.2 = (f32[256,64]{0,1:T(8,128)S(1)}, f32[256,64]{0,1:T(8,128)}, u32[]{:S(2)}) copy-start(f32[256,64]{0,1:T(8,128)} %param.10) | copy-start | bytes 196612
  27.0 35.8 %copy-start.3 = (f32[256,64]{0,1:T(8,128)S(1)}, f32[256,64]{0,1:T(8,128)}, u32[]{:S(2)}) copy-start(f32[256,64]{0,1:T(8,128)} %param.11) | copy-start | bytes 196612
  27.0 35.7 %copy-start.4 = (f32[64,64]{1,0:T(8,128)S(1)}, f32[64,64]{1,0:T(8,128)}, u32[]{:S(2)}) copy-start(f32[64,64]{1,0:T(8,128)} %param.12) | copy-start | bytes 49156
  27.0 35.7 %copy-start.5 = (f32[256]{0:T(256)S(1)}, f32[256]{0:T(256)}, u32[]{:S(2)}) copy-start(f32[256]{0:T(256)} %param.9) | copy-start | bytes 3076
  43.9 95.0 %all-reduce.9.cloned.1.call-start = ((), (), s32[]{:S(2)}) async-start(), calls=%async_computation.4 | async-start | bytes 524288 | tf_op jit(solution)/shard_map/psum | solution.py:54
  65.0 93.6 %all-reduce.7.cloned.1.call-start = ((), (), s32[]{:S(2)}) async-start(), calls=%async_computation.3 | async-start | bytes 131072 | tf_op jit(solution)/shard_map/psum | solution.py:66
Sparse Core Ops, SparseCore 0:
  10.6 22.8 reduce-scatter.1
  44.0 18.7 all-reduce.4
  66.2 72.6 all-reduce.8
  141.6 16.9 all-reduce.6
where the time goes:
time: 218 us
  blocking collectives  90.4 us (41%)
  waiting for transfers between devices  71.9 us (33%)
  matrix products  17.8 us (8%)
  other arithmetic  15.4 us (7%)
  between operations  13.9 us (6%)
  local copies, waits for them, and re-layouts  8.02 us (4%)
    psum x1, blocking collectives, local(): gram = lax.psum(gram_local, ('rows', 'cols')) / total_rows  37.4 us
    psum x1, blocking collectives, local(): lax.psum((diagonal_local, stored_local), ('rows', 'cols'))  37.4 us
    psum x1, waiting for transfers between devices, local(): correlation = lax.psum(correlation_local, ('rows', 'cols')) / total_rows  36.2 us
    psum x1, waiting for transfers between devices, apply_operator(): total = lax.psum(partial_total, 'sub')  18.8 us
    psum x1, waiting for transfers between devices, local(): removal = lax.psum(removal_local, 'sub')  16.8 us
    all_gather x1, blocking collectives, apply_operator(): gathered = lax.all_gather(own_tiles, 'rows', axis=0, tiled=True)  15.6 us
    dot_general x1, matrix products, apply_operator(): jnp.einsum('tk,kan->tan', row_onehot, pulled, precision=highest)  8.95 us
    another operation x3, other arithmetic, local(): lower_factor = jnp.linalg.cholesky(gram)  6.52 us
  transfers between devices with their start and end apart: 4, of which 3 were waited for; matrix products, arithmetic and copies ran while one was open for 8% of the time, Pallas kernels for 0%

commit v1 on v0

--- a/solution.py
+++ b/solution.py
@@ -63,7 +63,8 @@
     )
     images = images - jnp.dot(start_block, diagonal, precision=highest)
     removal_local = jnp.einsum("kib,kbc->ic", stored_basis, projection, precision=highest)
-    removal = lax.psum(removal_local, "sub")
+    shards = lax.all_gather(removal_local, "sub")
+    removal = jnp.sum(shards, axis=0)
     images = images - removal
     gram_local = jnp.dot(images.T, images, precision=highest)
     gram = lax.psum(gram_local, ("rows", "cols")) / total_rows

time: 218 us -> 232 us (1.064)
  waiting for transfers between devices: 71.9 us -> 86.9 us
    psum x1, waiting for transfers between devices: 36.2 us -> 68 us  [local(): correlation = lax.psum(correlation_local, ('rows', 'cols')) / total_rows]
    psum x1 -> x0, waiting for transfers between devices: 16.8 us -> none  [local(): removal = lax.psum(removal_local, 'sub')]
  transfers between devices with their start and end apart: 4 -> 3, of which waited for: 3 -> 2; matrix products, arithmetic and copies ran while one was open for 8% -> 7% of each run, Pallas kernels for 0% -> 0%
where the time goes in v1:
time: 232 us; the launch traced here: 231 us
  blocking collectives  90.3 us (39%)
  waiting for transfers between devices  86.9 us (37%)
  matrix products  16.3 us (7%)
  other arithmetic  15.5 us (7%)
  between operations  13.9 us (6%)
  local copies, waits for them, and re-layouts  8.11 us (3%)
    psum x1, waiting for transfers between devices, local(): correlation = lax.psum(correlation_local, ('rows', 'cols')) / total_rows  68 us
    psum x1, blocking collectives, local(): lax.psum((diagonal_local, stored_local), ('rows', 'cols'))  37.4 us
    psum x1, blocking collectives, local(): gram = lax.psum(gram_local, ('rows', 'cols')) / total_rows  35.4 us
    psum x1, waiting for transfers between devices, apply_operator(): total = lax.psum(partial_total, 'sub')  18.8 us
    all_gather x1, blocking collectives, apply_operator(): gathered = lax.all_gather(own_tiles, 'rows', axis=0, tiled=True)  15.6 us
    dot_general x1, matrix products, apply_operator(): jnp.einsum('tk,kan->tan', row_onehot, pulled, precision=highest)  8.95 us
    another operation x3, other arithmetic, local(): lower_factor = jnp.linalg.cholesky(gram)  6.52 us
    dot_general x1, local copies, waits for them, and re-layouts, apply_operator(): jnp.einsum('tk,kan->tan', row_onehot, pulled, precision=highest)  5.19 us
  transfers between devices with their start and end apart: 3, of which 2 were waited for; matrix products, arithmetic and copies ran while one was open for 7% of the time, Pallas kernels for 0%

profile of v1, /device:TPU:0, one launch (start us, length us, event | category | flops | bytes accessed | tf_op | source)
XLA Modules:
  0.0 231.2 jit_solution(10343153231105846824)
XLA Ops:
  7.2 0.9 convert_element_type.2
  8.1 0.9 fusion.27
  9.0 0.2 fusion.15
  9.2 0.5 fusion.5
  9.7 0.8 copy.31
  10.6 15.6 %all-gather = bf16[1024,64]{0,1:T(8,128)(2,1)S(1)} all-gather(bf16[256,64]{0,1:T(8,128)(2,1)S(1)} %convert_element_type.2), channel_id=2, replica_groups=mesh['groups'=2,'rows'=4,'cols'=2,'sub'=2] {'rows'}, dimensions={0}, use_global_device_ids=true | all-gather | bytes 163840 | tf_op jit(solution)/shard_map/all_gather | solution.py:21
  26.2 0.6 gather_fusion
  26.8 0.2 convolution_bitcast_fusion.1
  27.0 9.0 %fusion.3 = f32[1,256,64]{0,1,2:T(8,128)} fusion(f32[2,256,64]{1,2,0:T(8,128)S(1)} %convolution_bitcast_fusion.1), kind=kOutput, calls=%fused_computation.13 | convolution fusion | flops 393216 | bytes 196608 | tf_op jit(solution)/shard_map/tk,kan->tan/dot_general | solution.py:36
  36.0 5.2 %copy.42 = f32[1,256,64]{1,2,0:T(8,128)S(1)} copy(f32[1,256,64]{0,1,2:T(8,128)} %fusion.3) | data formatting | bytes 131072 | tf_op jit(solution)/shard_map/tk,kan->tan/dot_general | solution.py:36
  41.2 1.2 fusion.8
  42.4 1.5 add_bitcast_fusion
  43.9 18.8 %all-reduce.4.cloned.1.call-done = f32[256,64]{0,1:T(8,128)} async-done(((f32[256,64]{0,1:T(8,128)}), f32[256,64]{0,1:T(8,128)}) %all-reduce.4.cloned.1.call-update) | async-done | bytes 65552 | tf_op jit(solution)/shard_map/psum | solution.py:37
  62.8 1.1 fusion.2
  63.9 0.2 convolution_bitcast_fusion.6
  64.1 1.2 convolution_bitcast_fusion
  65.2 37.4 %psum.36 = f32[64,64]{0,1:T(8,128)S(1)} all-reduce(f32[64,64]{0,1:T(8,128)S(1)} %convolution_bitcast_fusion.6), channel_id=1, replica_groups=mesh['groups'=2,'rows'=4,'cols'=2,'sub'=2] {'rows','cols'}, use_global_device_ids=true, to_apply=%region_2.3 | all-reduce | flops 4096 | bytes 32768 | tf_op jit(solution)/shard_map/psum | solution.py:59
  102.7 0.7 copy.39
  103.4 68.0 %all-reduce.6.cloned.1.call-done = (f32[4,64,64]{1,2,0:T(8,128)}, f32[4,64,64]{1,2,0:T(8,128)}) async-done(((f32[4,64,64]{1,2,0:T(8,128)}, f32[4,64,64]{1,2,0:T(8,128)}), (f32[4,64,64]{1,2,0:T(8,128)}, f32[4,64,64]{1,2,0:T(8,128)})) %all-reduce.6.cloned.1.call-update) | async-done | bytes 131088 | tf_op jit(solution)/shard_map/psum | solution.py:54
  171.4 1.2 convolution_subtract_fusion
  172.6 0.3 convolution_bitcast_fusion.5
  172.9 1.9 all-gather.1
  174.9 0.2 reduce_sum.9
  175.1 0.2 fusion.1
  175.3 0.2 fusion.35
  175.5 35.4 %psum.39 = f32[64,64]{0,1:T(8,128)S(1)} all-reduce(f32[64,64]{0,1:T(8,128)S(1)} %fusion.35), channel_id=1, replica_groups=mesh['groups'=2,'rows'=4,'cols'=2,'sub'=2] {'rows','cols'}, use_global_device_ids=true, to_apply=%region_6.7 | all-reduce | flops 4096 | bytes 32768 | tf_op jit(solution)/shard_map/psum | solution.py:70
  211.0 5.8 %cholesky.15 = f32[64,64]{1,0:T(8,128)S(1)} custom-call(f32[64,64]{1,0:T(8,128)S(1)} %fusion.13), custom_call_target="Cholesky" | custom-call | tf_op jit(solution)/shard_map/jit(cholesky)/cholesky | solution.py:71
  216.9 0.6 compare_reduce_fusion
  217.6 0.7 fusion.20
  218.2 4.9 %custom-call.6 = f32[1,64,64]{1,2,0:T(8,128)S(1)} custom-call(f32[1,64,64]{2,1,0:T(8,128)S(1)} %get-tuple-element.20), custom_call_target="InvertDiagBlocksLowerTriangular" | custom-call | tf_op jit(solution)/shard_map/triangular_solve | solution.py:72
  223.1 0.9 convolution_bitcast_fusion.2
  224.0 0.7 copy.40
  (29 shorter events, 0.5 us)
Async XLA Ops:
  7.2 1.9 copy-start
  7.2 35.2 %reduce-scatter.2.cloned.1.call-start = ((), (), s32[]{:S(2)}) async-start(), calls=%async_computation.1 | async-start | bytes 327680 | tf_op jit(solution)/shard_map/reduce_scatter | solution.py:32
  10.5 52.2 %all-reduce.4.cloned.1.call-start = ((), (), s32[]{:S(2)}) async-start(), calls=%async_computation.2 | async-start | bytes 131072 | tf_op jit(solution)/shard_map/psum | solution.py:37
  27.0 14.2 %copy-start.1 = (f32[4,256,64]{1,2,0:T(8,128)S(1)}, f32[4,256,64]{1,2,0:T(8,128)}, u32[]{:S(2)}) copy-start(f32[4,256,64]{1,2,0:T(8,128)} %param.13) | copy-start | bytes 786436
  27.0 14.2 %copy-start.2 = (f32[256,64]{0,1:T(8,128)S(1)}, f32[256,64]{0,1:T(8,128)}, u32[]{:S(2)}) copy-start(f32[256,64]{0,1:T(8,128)} %param.10) | copy-start | bytes 196612
  27.0 35.8 %copy-start.3 = (f32[256,64]{0,1:T(8,128)S(1)}, f32[256,64]{0,1:T(8,128)}, u32[]{:S(2)}) copy-start(f32[256,64]{0,1:T(8,128)} %param.11) | copy-start | bytes 196612
  27.0 35.7 %copy-start.4 = (f32[64,64]{1,0:T(8,128)S(1)}, f32[64,64]{1,0:T(8,128)}, u32[]{:S(2)}) copy-start(f32[64,64]{1,0:T(8,128)} %param.12) | copy-start | bytes 49156
  27.0 35.7 %copy-start.5 = (f32[256]{0:T(256)S(1)}, f32[256]{0:T(256)}, u32[]{:S(2)}) copy-start(f32[256]{0:T(256)} %param.9) | copy-start | bytes 3076
  43.9 127.5 %all-reduce.6.cloned.1.call-start = ((), (), s32[]{:S(2)}) async-start(), calls=%async_computation.3 | async-start | bytes 524288 | tf_op jit(solution)/shard_map/psum | solution.py:54
Sparse Core Ops, SparseCore 0:
  10.6 22.8 reduce-scatter.1
  44.0 18.7 all-reduce.3
  102.8 68.5 all-reduce.5
